TPU v7x, 32 devices: a whole 2x2x4 slice. The times are simulated.
32 devices in a mesh: gy: 16 (over z, y, core), gz: 2 (over x).
Axes of the slice: x: 2, y: 2, z: 4, core: 2. Of those that a mesh axis runs over, the one named last changes fastest.
Arguments:
- scalar: float32 [8, 384, 384], P('gz', 'gy'), may hold values from -6 to 6
- velocity: float32 [3, 8, 128, 128], P(None, None, 'gy', 'gz'), may hold values from -0.9 to 0.9
Outputs:
- remeshed: float32 [8, 384, 384], P('gz', 'gy')
All inputs are finite; a program needn't handle non-finite values.
Results may differ from a plain program's by a relative error of at most 0.0003.
Values sent between devices are 32-bit elements; how exact they have to be, the bound alone decides.
A program may use at most 64 MiB of HBM per device.

v0:
```python
import jax
import jax.numpy as jnp
from jax import lax
from jax.sharding import PartitionSpec as P


def padded_2(value, sides, width):
    for axis, dim in sides:
        peers, length = (lax.axis_size(axis), value.shape[dim])
        up = [(i, (i + 1) % peers) for i in range(peers - 1)]
        down = [(j, i) for i, j in up]
        last = lax.slice_in_dim(value, length - width, length, axis=dim)
        initial = lax.slice_in_dim(value, 0, width, axis=dim)
        before = lax.ppermute(last, axis, up)
        after = lax.ppermute(initial, axis, down)
        value = jnp.concatenate([before, value, after], axis=dim)
    return value


def passed_along(block, axis, distance):
    devices = range(lax.axis_size(axis))
    route = [((i - distance) % len(devices), i) for i in devices]
    return lax.ppermute(block, axis, route)


def alternate(current, following, along):
    pieces = [current * (1.0 - phase / 3.0) + following * (phase / 3.0) for phase in range(3)]
    stacked = jnp.stack(pieces, axis=along + 1)
    new_shape = list(current.shape)
    new_shape[along] = new_shape[along] * 3
    return stacked.reshape(new_shape)


def polynomial(factors, value):
    result = jnp.zeros_like(value)
    for factor in reversed(factors):
        result = result * value + factor
    return result


def kernel_weight(offset):
    size = jnp.abs(offset)
    inner = polynomial([1.0, 0.0, -5.0 / 4.0, -35.0 / 12.0, 21.0 / 4.0, -25.0 / 12.0], size)
    middle = polynomial(
        [-4.0, 75.0 / 4.0, -245.0 / 8.0, 545.0 / 24.0, -63.0 / 8.0, 25.0 / 24.0], size
    )
    outer = polynomial(
        [18.0, -153.0 / 4.0, 255.0 / 8.0, -313.0 / 24.0, 21.0 / 8.0, -5.0 / 24.0], size
    )
    return jnp.where(
        size < 1.0, inner, jnp.where(size < 2.0, middle, jnp.where(size < 3.0, outer, 0.0))
    )


def displacement(speed, before, after):
    half_step = 0.5 * speed
    return jnp.where(
        half_step >= 0.0,
        (1.0 - half_step) * speed + half_step * after,
        (1.0 + half_step) * speed - half_step * before,
    )


def sweep_periodic(field, speed, along):
    moved = displacement(speed, jnp.roll(speed, 1, along), jnp.roll(speed, -1, along))
    result = jnp.zeros_like(field)
    for offset in range(-3, 4):
        result = result + jnp.roll(field * kernel_weight(offset - moved), offset, along)
    return result


def sweep_open(field, speed, padded):
    padded = padded_2(speed, (("gz", 0),), 1)
    moved = displacement(speed, padded[:-2], padded[2:])
    count = field.shape[0]
    total = jnp.zeros((count + 6,) + field.shape[1:], jnp.float32)
    for offset in range(-3, 4):
        total = total.at[3 + offset : 3 + offset + count].add(field * kernel_weight(offset - moved))
    ghosts = jnp.concatenate([total[:3], total[count + 3 :]], axis=0)
    received = padded_2(ghosts, (("gz", 0),), 3)
    result = total[3 : count + 3]
    result = result.at[:3].add(received[:3])
    result = result.at[count - 3 :].add(received[9:])
    return result


def local(scalar, velocity):
    coarse = lax.all_to_all(velocity, "gz", split_axis=1, concat_axis=3, tiled=True)
    rows_part = coarse[:1]
    next_row = passed_along(rows_part[:, :, :1, :], "gy", -1)
    y_fine = alternate(rows_part, jnp.concatenate([rows_part[:, :, 1:, :], next_row], axis=2), 2)
    fine_vel = alternate(y_fine, jnp.roll(y_fine, -1, 3), 3)
    field = sweep_periodic(scalar, fine_vel[0], 2)
    turned = jnp.swapaxes(field, 1, 2)
    padded_z = None
    sending = coarse[1:]
    field = lax.all_to_all(turned, "gy", split_axis=1, concat_axis=2, tiled=True)
    coarse_rows = jnp.swapaxes(sending, 2, 3)
    coarse_turned = lax.all_to_all(coarse_rows, "gy", split_axis=2, concat_axis=3, tiled=True)
    y_refined = alternate(coarse_turned, jnp.roll(coarse_turned, -1, 3), 3)
    next_col = passed_along(y_refined[:, :, :1, :], "gy", -1)
    pencil_vel = alternate(
        y_refined, jnp.concatenate([y_refined[:, :, 1:, :], next_col], axis=2), 2
    )
    speed_y = pencil_vel[0]
    speed_z = pencil_vel[1]
    field = sweep_periodic(field, speed_y, 2)
    return sweep_open(field, speed_z, padded_z)


def solution(mesh):
    in_specs = (P("gz", "gy", None), P(None, None, "gy", "gz"))
    out_specs = P("gz", "gy", None)
    return jax.shard_map(local, mesh=mesh, in_specs=in_specs, out_specs=out_specs, check_vma=False)
```

profile of v0, /device:TPU:0, one launch (start us, length us, event | category | flops | bytes accessed | tf_op | source)
XLA Modules:
  0.0 67.6 jit_solution(13665253573162339864)
XLA Ops:
  0.0 0.9 %copy.405 = f32[3,8,8,64]{3,2,0,1:T(8,128)S(1)} copy(f32[3,8,8,64]{3,2,1,0:T(8,128)} %param.21) | data formatting | bytes 98304 | tf_op args[1]
  1.0 8.1 %all_to_all.54 = f32[2,1,6144]{2,1,0:T(1,128)S(1)} all-to-all(f32[2,1,6144]{2,1,0:T(1,128)S(1)} %reshape.847), channel_id=1, replica_groups=mesh['gy'=16,'gz'=2] {'gz'}, dimensions={0} | all-to-all | bytes 98304 | tf_op jit(solution)/shard_map/all_to_all | solution.py:88
  9.6 0.8 %reduce.18 = f32[2,6144]{1,0:T(2,128)S(1)} reduce(f32[2,1,6144]{2,1,0:T(1,128)S(1)} %all_to_all.54, f32[]{:T(128)} %broadcast.909), dimensions={1}, to_apply=%all_to_all.39.reduce_sub_computation | reduce | bytes 98308 | tf_op jit(solution)/shard_map/all_to_all | solution.py:88
  10.7 2.7 %collective-permute-start = (f32[1,4,1,128]{3,2,1,0:T(1,128)S(1)}, f32[1,4,1,128]{3,2,1,0:T(1,128)S(1)}, u32[]{:S(2)}, u32[]{:S(2)}) collective-permute-start(f32[1,4,1,128]{3,2,1,0:T(1,128)S(1)} %slice.470), channel_id=1, source_target_pairs={{2,0},{4,2},{6,4},{8,6},{10,8},{12,10},{14,12},{16,14},{18,16},{20... | collective-permute-start | bytes 6152 | tf_op jit(solution)/shard_map/ppermute | solution.py:23
  13.8 1.1 %reshape.851 = f32[16,1,512]{2,1,0:T(1,128)} reshape(f32[128,2,4,8]{3,2,1,0:T(4,128)S(1)} %bitcast.81) | data formatting | bytes 65536
  15.0 3.5 %all-to-all-start.2 = ((f32[16,1,512]{2,1,0:T(1,128)}), f32[16,1,512]{2,1,0:T(1,128)S(1)}, u32[]{:S(2)}, u32[]{:S(2)}) async-start(f32[16,1,512]{2,1,0:T(1,128)} %reshape.851), calls=%async_computation.2 | async-start | bytes 65536 | tf_op jit(solution)/shard_map/all_to_all | solution.py:99
  20.2 1.0 %fusion.22 = (f32[4,24,384]{2,1,0:T(8,128)S(1)}, f32[4,24,384]{2,1,0:T(8,128)S(1)}, f32[4,24,384]{2,1,0:T(8,128)S(1)}, f32[4,24,384]{2,1,0:T(8,128)S(1)}, f32[4,24,384]{2,1,0:T(8,128)S(1)}) fusion(f32[4,24,384]{2,1,0:T(8,128)S(1)} %copy-done, f32[4,24,384]{2,1,0:T(8,128)S(1)} %get-tuple-element.121), kind=kLoop, calls=%fused_computation.47 | loop fusion | flops 7741440 | bytes 1032192 | tf_op jit(solution)/shard_map/mul | solution.py:68
  22.4 1.7 %reshape.849 = f32[16,1,2304]{2,1,0:T(1,128)} reshape(f32[384,4,24]{2,1,0:T(4,128)S(1)} %bitcast.78) | data formatting | bytes 294912
  24.1 1.0 %all-to-all-done.2 = f32[16,1,512]{2,1,0:T(1,128)S(1)} async-done(((f32[16,1,512]{2,1,0:T(1,128)}), f32[16,1,512]{2,1,0:T(1,128)S(1)}, u32[]{:S(2)}, u32[]{:S(2)}) %all-to-all-start.2) | async-done | bytes 32800 | tf_op jit(solution)/shard_map/all_to_all | solution.py:99
  25.1 4.9 %all-to-all-start.1 = ((f32[16,1,2304]{2,1,0:T(1,128)}), f32[16,1,2304]{2,1,0:T(1,128)S(1)}, u32[]{:S(2)}, u32[]{:S(2)}) async-start(f32[16,1,2304]{2,1,0:T(1,128)} %reshape.849), calls=%async_computation.1 | async-start | bytes 294912 | tf_op jit(solution)/shard_map/all_to_all | solution.py:97
  32.4 0.7 %copy.364 = f32[2,4,8,128,3]{2,1,4,3,0:T(4,128)S(1)} copy(f32[2,4,8,128,3]{3,2,1,0,4:T(8,128)S(1)} %pad_maximum_fusion.4) | data formatting | bytes 196608 | tf_op jit(solution)/shard_map/stack | solution.py:28
  33.8 4.4 %collective-permute-start.1 = (f32[2,4,1,384]{3,1,2,0:T(4,128)S(1)}, f32[2,4,1,384]{3,1,2,0:T(4,128)S(1)}, u32[]{:S(2)}, u32[]{:S(2)}) collective-permute-start(f32[2,4,1,384]{3,1,2,0:T(4,128)S(1)} %copy.366), channel_id=1, source_target_pairs={{2,0},{4,2},{6,4},{8,6},{10,8},{12,10},{14,12},{16,14},{18,16},{20... | collective-permute-start | bytes 36872 | tf_op jit(solution)/shard_map/ppermute | solution.py:23
  38.2 0.9 %slice_bitcast_fusion = f32[2,4,7,1,384]{2,1,4,0,3:T(4,128)S(1)} fusion(f32[2,4,8,384]{2,1,3,0:T(4,128)S(1)} %bitcast.70), kind=kLoop, calls=%fused_computation | loop fusion | bytes 172032 | tf_op jit(solution)/shard_map/concatenate | solution.py:103
  40.5 2.2 %collective-permute-start.3 = (f32[1,24,384]{2,0,1:T(1,128)S(1)}, f32[1,24,384]{2,0,1:T(1,128)S(1)}, u32[]{:S(2)}, u32[]{:S(2)}) collective-permute-start(f32[1,24,384]{2,0,1:T(1,128)S(1)} %bitcast.97), channel_id=1, source_target_pairs={{0,1},{2,3},{4,5},{6,7},{8,9},{10,11},{12,13},{14,15},{16,17},{18,... | collective-permute-start | bytes 110600 | tf_op jit(solution)/shard_map/ppermute | solution.py:14
  42.8 1.5 %collective-permute-start.2 = (f32[1,24,384]{2,0,1:T(1,128)S(1)}, f32[1,24,384]{2,0,1:T(1,128)S(1)}, u32[]{:S(2)}, u32[]{:S(2)}) collective-permute-start(f32[1,24,384]{2,0,1:T(1,128)S(1)} %bitcast.98), channel_id=1, source_target_pairs={{1,0},{3,2},{5,4},{7,6},{9,8},{11,10},{13,12},{15,14},{17,16},{19,... | collective-permute-start | bytes 110600 | tf_op jit(solution)/shard_map/ppermute | solution.py:15
  44.7 3.9 %collective-permute-done.2 = f32[1,24,384]{2,0,1:T(1,128)S(1)} collective-permute-done((f32[1,24,384]{2,0,1:T(1,128)S(1)}, f32[1,24,384]{2,0,1:T(1,128)S(1)}, u32[]{:S(2)}, u32[]{:S(2)}) %collective-permute-start.2) | collective-permute-done | bytes 36896 | tf_op jit(solution)/shard_map/ppermute | solution.py:15
  48.6 1.0 %reduce.20 = f32[16,2304]{1,0:T(8,128)S(1)} reduce(f32[16,1,2304]{2,1,0:T(1,128)S(1)} %all-to-all-done.1, f32[]{:T(128)} %broadcast.909), dimensions={1}, to_apply=%all_to_all.42.reduce_sub_computation | reduce | bytes 294916 | tf_op jit(solution)/shard_map/all_to_all | solution.py:97
  49.6 1.1 %reshape.850 = f32[384,4,24]{2,1,0:T(4,128)S(1)} reshape(f32[16,2304]{1,0:T(8,128)S(1)} %reduce.20) | data formatting | bytes 294912
  51.9 1.0 %fusion.28 = (f32[4,24,384]{2,1,0:T(8,128)S(1)}, f32[4,24,384]{2,1,0:T(8,128)S(1)}, f32[4,24,384]{2,1,0:T(8,128)S(1)}, f32[4,24,384]{2,1,0:T(8,128)S(1)}, f32[4,24,384]{2,1,0:T(8,128)S(1)}) fusion(f32[4,24,384]{2,1,0:T(8,128)S(1)} %all_to_all.45, f32[4,24,384]{2,1,0:T(8,128)S(1)} %get-tuple-element.119), kind=kLoop, calls=%fused_computation.53 | loop fusion | flops 7741440 | bytes 1032192 | tf_op jit(solution)/shard_map/mul | solution.py:68
  55.4 1.6 %collective-permute-start.4 = (f32[3,24,384]{2,1,0:T(8,128)S(1)}, f32[3,24,384]{2,1,0:T(8,128)S(1)}, u32[]{:S(2)}, u32[]{:S(2)}) collective-permute-start(f32[3,24,384]{2,1,0:T(8,128)S(1)} %slice.519), channel_id=1, source_target_pairs={{0,1},{2,3},{4,5},{6,7},{8,9},{10,11},{12,13},{14,15},{16,17},{18,... | collective-permute-start | bytes 331784 | tf_op jit(solution)/shard_map/ppermute | solution.py:14
  57.1 2.3 %collective-permute-done.4 = f32[3,24,384]{2,1,0:T(8,128)S(1)} collective-permute-done((f32[3,24,384]{2,1,0:T(8,128)S(1)}, f32[3,24,384]{2,1,0:T(8,128)S(1)}, u32[]{:S(2)}, u32[]{:S(2)}) %collective-permute-start.4) | collective-permute-done | bytes 110624 | tf_op jit(solution)/shard_map/ppermute | solution.py:14
  59.4 1.3 %collective-permute-start.5 = (f32[3,24,384]{2,1,0:T(8,128)S(1)}, f32[3,24,384]{2,1,0:T(8,128)S(1)}, u32[]{:S(2)}, u32[]{:S(2)}) collective-permute-start(f32[3,24,384]{2,1,0:T(8,128)S(1)} %get-tuple-element.122), channel_id=1, source_target_pairs={{1,0},{3,2},{5,4},{7,6},{9,8},{11,10},{13,12},{15,14},{17,16},{19,... | collective-permute-start | bytes 331784 | tf_op jit(solution)/shard_map/ppermute | solution.py:15
  60.7 5.3 %collective-permute-done.5 = f32[3,24,384]{2,1,0:T(8,128)S(1)} collective-permute-done((f32[3,24,384]{2,1,0:T(8,128)S(1)}, f32[3,24,384]{2,1,0:T(8,128)S(1)}, u32[]{:S(2)}, u32[]{:S(2)}) %collective-permute-start.5) | collective-permute-done | bytes 110624 | tf_op jit(solution)/shard_map/ppermute | solution.py:15
  66.0 1.6 %fusion.226 = f32[4,24,384]{2,1,0:T(8,128)} fusion(f32[4,24,384]{2,1,0:T(8,128)} %copy-done.1, f32[3,24,384]{2,1,0:T(8,128)S(1)} %collective-permute-done.5), kind=kLoop, calls=%fused_computation.310 | loop fusion | flops 27648 | bytes 331776 | tf_op jit(solution)/shard_map/scatter-add | solution.py:83
  (97 shorter events, 12.6 us)
Async XLA Ops:
  10.7 7.8 %collective-permute-start = (f32[1,4,1,128]{3,2,1,0:T(1,128)S(1)}, f32[1,4,1,128]{3,2,1,0:T(1,128)S(1)}, u32[]{:S(2)}, u32[]{:S(2)}) collective-permute-start(f32[1,4,1,128]{3,2,1,0:T(1,128)S(1)} %slice.470), channel_id=1, source_target_pairs={{2,0},{4,2},{6,4},{8,6},{10,8},{12,10},{14,12},{16,14},{18,16},{20... | collective-permute-start | bytes 6152 | tf_op jit(solution)/shard_map/ppermute | solution.py:23
  15.0 10.1 %all-to-all-start.2 = ((f32[16,1,512]{2,1,0:T(1,128)}), f32[16,1,512]{2,1,0:T(1,128)S(1)}, u32[]{:S(2)}, u32[]{:S(2)}) async-start(f32[16,1,512]{2,1,0:T(1,128)} %reshape.851), calls=%async_computation.2 | async-start | bytes 65536 | tf_op jit(solution)/shard_map/all_to_all | solution.py:99
  18.9 1.0 %copy-start = (f32[4,24,384]{2,1,0:T(8,128)S(1)}, f32[4,24,384]{2,1,0:T(8,128)}, u32[]{:S(2)}) copy-start(f32[4,24,384]{2,1,0:T(8,128)} %param.20) | copy-start | bytes 442372
  25.1 23.6 %all-to-all-start.1 = ((f32[16,1,2304]{2,1,0:T(1,128)}), f32[16,1,2304]{2,1,0:T(1,128)S(1)}, u32[]{:S(2)}, u32[]{:S(2)}) async-start(f32[16,1,2304]{2,1,0:T(1,128)} %reshape.849), calls=%async_computation.1 | async-start | bytes 294912 | tf_op jit(solution)/shard_map/all_to_all | solution.py:97
  33.8 6.5 %collective-permute-start.1 = (f32[2,4,1,384]{3,1,2,0:T(4,128)S(1)}, f32[2,4,1,384]{3,1,2,0:T(4,128)S(1)}, u32[]{:S(2)}, u32[]{:S(2)}) collective-permute-start(f32[2,4,1,384]{3,1,2,0:T(4,128)S(1)} %copy.366), channel_id=1, source_target_pairs={{2,0},{4,2},{6,4},{8,6},{10,8},{12,10},{14,12},{16,14},{18,16},{20... | collective-permute-start | bytes 36872 | tf_op jit(solution)/shard_map/ppermute | solution.py:23
  40.5 4.2 %collective-permute-start.3 = (f32[1,24,384]{2,0,1:T(1,128)S(1)}, f32[1,24,384]{2,0,1:T(1,128)S(1)}, u32[]{:S(2)}, u32[]{:S(2)}) collective-permute-start(f32[1,24,384]{2,0,1:T(1,128)S(1)} %bitcast.97), channel_id=1, source_target_pairs={{0,1},{2,3},{4,5},{6,7},{8,9},{10,11},{12,13},{14,15},{16,17},{18,... | collective-permute-start | bytes 110600 | tf_op jit(solution)/shard_map/ppermute | solution.py:14
  42.8 5.9 %collective-permute-start.2 = (f32[1,24,384]{2,0,1:T(1,128)S(1)}, f32[1,24,384]{2,0,1:T(1,128)S(1)}, u32[]{:S(2)}, u32[]{:S(2)}) collective-permute-start(f32[1,24,384]{2,0,1:T(1,128)S(1)} %bitcast.98), channel_id=1, source_target_pairs={{1,0},{3,2},{5,4},{7,6},{9,8},{11,10},{13,12},{15,14},{17,16},{19,... | collective-permute-start | bytes 110600 | tf_op jit(solution)/shard_map/ppermute | solution.py:15
  55.4 3.9 %collective-permute-start.4 = (f32[3,24,384]{2,1,0:T(8,128)S(1)}, f32[3,24,384]{2,1,0:T(8,128)S(1)}, u32[]{:S(2)}, u32[]{:S(2)}) collective-permute-start(f32[3,24,384]{2,1,0:T(8,128)S(1)} %slice.519), channel_id=1, source_target_pairs={{0,1},{2,3},{4,5},{6,7},{8,9},{10,11},{12,13},{14,15},{16,17},{18,... | collective-permute-start | bytes 331784 | tf_op jit(solution)/shard_map/ppermute | solution.py:14
  59.4 6.7 %copy-start.1 = (f32[4,24,384]{2,1,0:T(8,128)}, f32[4,24,384]{2,1,0:T(8,128)S(1)}, u32[]{:S(2)}) copy-start(f32[4,24,384]{2,1,0:T(8,128)S(1)} %get-tuple-element.123) | copy-start | bytes 442372
  59.4 6.6 %collective-permute-start.5 = (f32[3,24,384]{2,1,0:T(8,128)S(1)}, f32[3,24,384]{2,1,0:T(8,128)S(1)}, u32[]{:S(2)}, u32[]{:S(2)}) collective-permute-start(f32[3,24,384]{2,1,0:T(8,128)S(1)} %get-tuple-element.122), channel_id=1, source_target_pairs={{1,0},{3,2},{5,4},{7,6},{9,8},{11,10},{13,12},{15,14},{17,16},{19,... | collective-permute-start | bytes 331784 | tf_op jit(solution)/shard_map/ppermute | solution.py:15
where the time goes:
time: 68 us; the launch traced here: 67.6 us
  starting transfers between devices  22.1 us (32%)
  local copies, waits for them, and re-layouts  15.1 us (22%)
  waiting for transfers between devices  12.6 us (19%)
  other arithmetic  9.22 us (14%)
  blocking collectives  8.07 us (12%)
    ppermute x2, waiting for transfers between devices, padded_2(): after = lax.ppermute(initial, axis, down)  9.27 us
    all_to_all x1, blocking collectives, local(): lax.all_to_all(velocity, 'gz', split_axis=1, concat_axis=3, tiled=True)  8.07 us
    ppermute x2, starting transfers between devices, passed_along(): return lax.ppermute(block, axis, route)  7.05 us
    unnamed x15, local copies, waits for them, and re-layouts  5.7 us
    all_to_all x1, starting transfers between devices, local(): lax.all_to_all(turned, 'gy', split_axis=1, concat_axis=2, tiled=True)  4.95 us
    ppermute x2, starting transfers between devices, padded_2(): before = lax.ppermute(last, axis, up)  3.81 us
    all_to_all x1, starting transfers between devices, local(): lax.all_to_all(coarse_rows, 'gy', split_axis=2, concat_axis=3, tiled=True)  3.49 us
    ppermute x2, starting transfers between devices, padded_2(): after = lax.ppermute(initial, axis, down)  2.76 us
  transfers between devices with their start and end apart: 8, of which 4 were waited for; matrix products, arithmetic and copies ran while one was open for 19% of the time, Pallas kernels for 0%

commit v1 on v0

v1 whole, which is shorter than its diff:
```python
import functools

import jax
import jax.numpy as jnp
import numpy as np
from jax import lax
from jax.experimental import pallas as pl
from jax.experimental.pallas import tpu as pltpu
from jax.sharding import PartitionSpec as P

LANES = 128
INNER = [1.0, 0.0, -5.0 / 4.0, -35.0 / 12.0, 21.0 / 4.0, -25.0 / 12.0]
MIDDLE = [-4.0, 75.0 / 4.0, -245.0 / 8.0, 545.0 / 24.0, -63.0 / 8.0, 25.0 / 24.0]
OUTER = [18.0, -153.0 / 4.0, 255.0 / 8.0, -313.0 / 24.0, 21.0 / 8.0, -5.0 / 24.0]


def shifted(factors, base, slope):
    total = np.polynomial.Polynomial([0.0])
    for factor in reversed(factors):
        total = total * np.polynomial.Polynomial([base, slope]) + factor
    coefs = np.zeros(6)
    coefs[: len(total.coef)] = total.coef
    return [0.0 if abs(c) < 1e-10 else float(c) for c in coefs]


AHEAD = {1: shifted(INNER, 1.0, -1.0), 2: shifted(MIDDLE, 2.0, -1.0), 3: shifted(OUTER, 3.0, -1.0)}
BEHIND = {1: shifted(MIDDLE, 1.0, 1.0), 2: shifted(OUTER, 2.0, 1.0)}


def horner(factors, value):
    lowest = 0
    while factors[lowest] == 0.0:
        lowest += 1
    result = jnp.full_like(value, factors[-1])
    for factor in reversed(factors[lowest:-1]):
        result = result * value
        if factor != 0.0:
            result = result + factor
    for _ in range(lowest):
        result = result * value
    return result


def weights(moved):
    size = jnp.abs(moved)
    positive = moved >= 0.0
    result = {0: horner(INNER, size)}
    for m in (1, 2, 3):
        near = horner(AHEAD[m], size)
        far = horner(BEHIND[m], size) if m in BEHIND else jnp.zeros_like(size)
        result[m] = jnp.where(positive, near, far)
        result[-m] = jnp.where(positive, far, near)
    return result


def displacement(speed, before, after):
    return speed + 0.5 * speed * jnp.where(speed >= 0.0, after - speed, speed - before)


def roll(value, shift, axis):
    return pltpu.roll(value, shift % value.shape[axis], axis)


def sweep_periodic(field, speed, axis):
    moved = displacement(speed, roll(speed, 1, axis), roll(speed, -1, axis))
    w = weights(moved)
    result = field * w[0]
    for m in (-3, -2, -1, 1, 2, 3):
        result = result + roll(field * w[m], m, axis)
    return result


def dot(a, b, dims=((1,), (0,))):
    return lax.dot_general(
        a, b, (dims, ((), ())), precision=lax.Precision.HIGHEST, preferred_element_type=jnp.float32
    )


def refine(coarse):
    out = np.zeros((coarse, 3 * coarse), np.float32)
    for c in range(coarse):
        for k in range(3):
            out[c, 3 * c + k] += 1.0 - k / 3.0
            out[(c + 1) % coarse, 3 * c + k] += k / 3.0
    return out


def refine_block(count):
    out = np.zeros((2 * count, 3 * count), np.float32)
    for c in range(count):
        for k in range(3):
            out[c, 3 * c + k] += 1.0 - k / 3.0
            out[c + 1, 3 * c + k] += k / 3.0
    return out


def constants(nz, gz, gy, yc, xc):
    bc = gz * xc // gy
    full = refine(gz * xc)
    ex = np.zeros((gz, LANES, full.shape[1]), np.float32)
    for h in range(gz):
        ex[h, :xc] = full[h * xc : (h + 1) * xc]
    block = refine_block(yc)
    rows = np.zeros((nz * 3 * yc, 2 * nz * yc), np.float32)
    for z in range(nz):
        for part in range(2):
            at = part * nz * yc + z * yc
            rows[z * 3 * yc : (z + 1) * 3 * yc, at : at + yc] = block[part * yc : (part + 1) * yc].T
    block = refine_block(bc)
    planes = 2 * nz + 2
    xy = np.zeros((2 * LANES, LANES), np.float32)
    xz = np.zeros(((nz + 2) * 3 * bc, 2 * LANES), np.float32)
    for plane in range(planes):
        for part in range(2):
            at = part * LANES + plane * bc
            piece = block[part * bc : (part + 1) * bc]
            if plane < nz:
                xy[at : at + bc, plane * 3 * bc : (plane + 1) * 3 * bc] = piece
            else:
                z = plane - nz
                xz[z * 3 * bc : (z + 1) * 3 * bc, at : at + bc] = piece.T
    ey = refine(gy * yc)
    return rows, ex, xy, xz, ey, np.ascontiguousarray(ey.T)


def kernel(gz, gy, nz, yc, xc, *refs):
    (scalar_hbm, vel, rows_hbm, ex_hbm, xy_hbm, xz_hbm, ey_hbm, eyt_hbm, out,
     scalar, rows_m, ex_m, xy_m, xz_m, ey_m, eyt_m,
     own, nxt, vsend, v0, v1, blocks, pencil, up_out, down_out, up_in, down_in,
     local_sem, own_s, own_r, nxt_s, nxt_r, v0_s, v0_r, v1_s, v1_r, blk_s, blk_r, z_s, z_r) = refs
    h = lax.axis_index("gz")
    s = lax.axis_index("gy")
    rf = 3 * yc
    bc = gz * xc // gy
    bf = 3 * bc
    per = gy // gz
    ahead = lax.rem(s + 1, gy)
    behind = lax.rem(s + gy - 1, gy)
    total = gz * nz

    loads = []
    for i, (src, dst) in enumerate((
        (scalar_hbm, scalar), (rows_hbm, rows_m), (ex_hbm, ex_m), (xy_hbm, xy_m),
        (xz_hbm, xz_m), (ey_hbm, ey_m), (eyt_hbm, eyt_m),
    )):
        load = pltpu.make_async_copy(src, dst, local_sem.at[i])
        load.start()
        loads.append(load)

    def remote(src, dst, send, recv, p, g):
        return pltpu.make_async_remote_copy(
            src_ref=src, dst_ref=dst, send_sem=send, recv_sem=recv,
            device_id={"gz": p, "gy": g}, device_id_type=pl.DeviceIdType.MESH,
        )

    def ux_copies(step):
        p = lax.rem(h + step, gz)
        planes = vel.at[0, pl.ds(p * nz, nz)]
        first = (
            pltpu.make_async_copy(planes, own.at[h], own_r.at[h])
            if step == 0
            else remote(planes, own.at[h], own_s.at[step], own_r.at[h], p, s)
        )
        return first, remote(planes, nxt.at[h], nxt_s.at[step], nxt_r.at[h], p, behind)

    ux = [ux_copies(step) for step in range(gz)]
    for first, second in ux:
        second.start()
        first.start()

    lane = lax.broadcasted_iota(jnp.int32, (yc, LANES), 1)
    for p in range(gz):
        planes = [vel[1, p * nz + z] for z in range(nz)]
        for z in range(p * nz - 1, p * nz + nz + 1):
            planes.append(vel[2, z] if 0 <= z < total else None)
        for c in range(per):
            tile = jnp.zeros((yc, LANES), jnp.float32)
            for i, plane in enumerate(planes):
                if plane is not None:
                    tile = jnp.where(
                        (lane >= i * bc) & (lane < (i + 1) * bc), roll(plane, (i - c) * bc, 1), tile
                    )
            vsend[p, c] = tile

    def v_copies(which, n, act, own_too):
        dst_buf, send, recv, back = ((v0, v0_s, v0_r, 0), (v1, v1_s, v1_r, 1))[which]
        p = n // per
        c = n % per
        g = lax.rem(h * per + c + gy - back, gy)
        mine = (p == h) & (g == s)

        @pl.when(jnp.logical_not(mine))
        def _():
            act(remote(vsend.at[p, c], dst_buf.at[s], send.at[n], recv.at[s], p, g))

        if own_too:
            @pl.when(mine)
            def _():
                act(pltpu.make_async_copy(vsend.at[p, c], dst_buf.at[s], recv.at[s]))

    for n in range(gz * per):
        for which in range(2):
            v_copies(which, n, lambda copy: copy.start(), True)

    loads[0].wait()
    loads[1].wait()
    loads[2].wait()
    count = nz * yc
    speed = None
    for i in range(gz):
        pltpu.make_async_copy(own.at[i], own.at[i], own_r.at[i]).wait()
        pltpu.make_async_copy(nxt.at[i], nxt.at[i], nxt_r.at[i]).wait()
        coarse = jnp.concatenate(
            [own[i].reshape(count, LANES), nxt[i].reshape(count, LANES)], axis=0
        )
        part = dot(dot(rows_m[...], coarse), ex_m[i])
        speed = part if speed is None else speed + part
    nx = scalar.shape[2]
    field = scalar[...].reshape(nz * rf, nx)
    field = sweep_periodic(field, speed, 1)

    wide = lax.broadcasted_iota(jnp.int32, (rf, LANES), 1)
    for g in range(gy):
        low = g * bf
        first, last = low // LANES, (low + bf - 1) // LANES
        tile = jnp.zeros((rf, LANES), jnp.float32)
        for z in range(nz):
            for t in range(first, last + 1):
                piece = field[z * rf : (z + 1) * rf, t * LANES : (t + 1) * LANES]
                begin = z * bf + max(0, t * LANES - low)
                end = z * bf + min(bf, (t + 1) * LANES - low)
                tile = jnp.where(
                    (wide >= begin) & (wide < end), roll(piece, z * bf - low, 1), tile
                )
        blocks[g] = tile

    def block_copy(step):
        g = lax.rem(s + step, gy)
        if step == 0:
            return pltpu.make_async_copy(blocks.at[g], pencil.at[s], blk_r.at[s])
        return remote(blocks.at[g], pencil.at[s], blk_s.at[step], blk_r.at[s], h, g)

    sends = [block_copy(step) for step in range(gy)]
    for copy in sends[1:] + sends[:1]:
        copy.start()

    for load in loads[3:]:
        load.wait()
    for i in range(gy):
        pltpu.make_async_copy(v0.at[i], v0.at[i], v0_r.at[i]).wait()
        pltpu.make_async_copy(v1.at[i], v1.at[i], v1_r.at[i]).wait()
    nyc = gy * yc
    coarse = jnp.concatenate(
        [v0[...].reshape(nyc, LANES), v1[...].reshape(nyc, LANES)], axis=1
    )
    speed_y = dot(eyt_m[...], dot(coarse, xy_m[...]))
    speed_z = dot(dot(xz_m[...], coarse, ((1,), (1,))), ey_m[...])

    for i in range(gy):
        pltpu.make_async_copy(pencil.at[i], pencil.at[i], blk_r.at[i]).wait()
    field = pencil[...].reshape(gy * rf, LANES)
    field = sweep_periodic(field, speed_y, 0)

    field = jnp.transpose(field)[: nz * bf]
    moved = displacement(
        speed_z[bf : (nz + 1) * bf], speed_z[: nz * bf], speed_z[2 * bf : (nz + 2) * bf]
    )
    w = weights(moved)

    def landing(target):
        result = None
        for m in range(-3, 4):
            z = target - m
            if 0 <= z < nz:
                at = slice(z * bf, (z + 1) * bf)
                term = field[at] * w[m][at]
                result = term if result is None else result + term
        return result

    for i in range(3):
        up_out[i] = landing(nz + i)
        down_out[i] = landing(i - 3)

    up = remote(up_out, up_in, z_s.at[0], z_r.at[0], lax.rem(h + 1, gz), s)
    down = remote(down_out, down_in, z_s.at[1], z_r.at[1], lax.rem(h + gz - 1, gz), s)

    @pl.when(h < gz - 1)
    def _():
        up.start()

    @pl.when(h > 0)
    def _():
        down.start()

    for i in range(nz):
        out[i] = landing(i)

    @pl.when(h > 0)
    def _():
        up.wait_recv()
        for i in range(3):
            out[i] = out[i] + up_in[i]
        down.wait_send()

    @pl.when(h < gz - 1)
    def _():
        down.wait_recv()
        for i in range(3):
            out[nz - 3 + i] = out[nz - 3 + i] + down_in[i]
        up.wait_send()

    for step, (first, second) in enumerate(ux):
        if step:
            first.wait_send()
        second.wait_send()
    for copy in sends[1:]:
        copy.wait_send()
    for n in range(gz * per):
        for which in range(2):
            v_copies(which, n, lambda copy: copy.wait_send(), False)


def local(scalar, velocity):
    gz, gy = lax.axis_size("gz"), lax.axis_size("gy")
    nz, rf, nx = scalar.shape
    yc, xc = velocity.shape[2:]
    bc = gz * xc // gy
    bf = 3 * bc
    ny = gy * rf
    vel = jnp.pad(velocity, ((0, 0), (0, 0), (0, 0), (0, LANES - xc)))
    mats = constants(nz, gz, gy, yc, xc)
    per = gy // gz
    f32 = jnp.float32
    dma = pltpu.SemaphoreType.DMA
    anywhere = pl.BlockSpec(memory_space=pl.ANY)
    vmem = pl.BlockSpec(memory_space=pltpu.VMEM)
    scratch = [pltpu.VMEM(scalar.shape, f32)]
    scratch += [pltpu.VMEM(m.shape, f32) for m in mats]
    scratch += [
        pltpu.VMEM((gz, nz, yc, LANES), f32),
        pltpu.VMEM((gz, nz, yc, LANES), f32),
        pltpu.VMEM((gz, per, yc, LANES), f32),
        pltpu.VMEM((gy, yc, LANES), f32),
        pltpu.VMEM((gy, yc, LANES), f32),
        pltpu.VMEM((gy, rf, LANES), f32),
        pltpu.VMEM((gy, rf, LANES), f32),
    ]
    scratch += [pltpu.VMEM((3, bf, ny), f32)] * 4
    scratch += [dma((n,)) for n in (
        1 + len(mats), gz, gz, gz, gz, gz * per, gy, gz * per, gy, gy, gy, 2, 2
    )]
    return pl.pallas_call(
        functools.partial(kernel, gz, gy, nz, yc, xc),
        out_shape=jax.ShapeDtypeStruct((nz, bf, ny), f32),
        in_specs=[anywhere, vmem] + [anywhere] * len(mats),
        out_specs=vmem,
        scratch_shapes=scratch,
        compiler_params=pltpu.CompilerParams(has_side_effects=True),
    )(scalar, vel, *[jnp.asarray(m) for m in mats])


def solution(mesh):
    in_specs = (P("gz", "gy", None), P(None, None, "gy", "gz"))
    out_specs = P("gz", "gy", None)
    return jax.shard_map(local, mesh=mesh, in_specs=in_specs, out_specs=out_specs, check_vma=False)
```

time: 68 us -> 30.2 us (0.44)
  Pallas kernels: 0 us -> 26.9 us
  starting transfers between devices: 22.1 us -> 0 us
  waiting for transfers between devices: 12.6 us -> 0 us
  local copies, waits for them, and re-layouts: 15.1 us -> 3.12 us
  other arithmetic: 9.22 us -> 0 us
  blocking collectives: 8.07 us -> 0 us
    pallas_call x0 -> x1, Pallas kernels: none -> 26.9 us  [local(): pl.pallas_call(functools.partial(kernel, gz, gy, nz, yc, xc), out_shape=j...]
    ppermute x6 -> x0, starting transfers between devices: 13.6 us -> none  [the longest x2 7.05 us: passed_along(): return lax.ppermute(block, axis, route)]
    ppermute x6 -> x0, waiting for transfers between devices: 11.6 us -> none  [the longest x2 9.27 us: padded_2(): after = lax.ppermute(initial, axis, down)]
    all_to_all x2 -> x0, starting transfers between devices: 8.44 us -> none  [the longest x1 4.95 us: local(): lax.all_to_all(turned, 'gy', split_axis=1, concat_axis=2, tiled=True)]
    all_to_all x1 -> x0, blocking collectives: 8.07 us -> none  [local(): lax.all_to_all(velocity, 'gz', split_axis=1, concat_axis=3, tiled=True)]
    unnamed x15 -> x1, local copies, waits for them, and re-layouts: 5.7 us -> 1.58 us
    mul x5 -> x0, other arithmetic: 3.25 us -> none  [the longest x4 2.68 us: sweep_periodic(): field * kernel_weight(offset - moved)]
    scatter-add x7 -> x0, other arithmetic: 2.86 us -> none  [the longest x1 1.56 us: sweep_open(): result = result.at[count - 3:].add(received[9:])]
  transfers between devices with their start and end apart: 8 -> 0, of which waited for: 4 -> 0; matrix products, arithmetic and copies ran while one was open for 19% -> 0% of each run, Pallas kernels for 0% -> 0%
where the time goes in v1:
time: 30.2 us; the launch traced here: 30 us
  Pallas kernels  26.9 us (89%)
  local copies, waits for them, and re-layouts  3.12 us (10%)
    pallas_call x1, Pallas kernels, local(): pl.pallas_call(functools.partial(kernel, gz, gy, nz, yc, xc), out_shape=j...  26.9 us
    unnamed x1, local copies, waits for them, and re-layouts  1.58 us
    pad x1, local copies, waits for them, and re-layouts, local(): vel = jnp.pad(velocity, ((0, 0), (0, 0), (0, 0), (0, LANES - xc)))  1.54 us

profile of v1, /device:TPU:0, one launch (start us, length us, event | category | flops | bytes accessed | tf_op | source)
XLA Modules:
  0.0 30.0 jit_solution(7219117662777129350)
XLA Ops:
  0.0 1.5 %pad.4.refs_1_ = f32[3,8,8,128]{3,2,1,0:T(8,128)} pad(f32[3,8,8,64]{3,2,1,0:T(8,128)} %param.9, f32[]{:T(128)} %constant.14.clone.1), padding=0_0x0_0x0_0x0_64 | pad | bytes 147460 | tf_op jit(solution)/shard_map/jit(_pad)/pad | solution.py:330
  1.5 26.9 %shard_map.82 = f32[4,24,384]{2,1,0:T(8,128)} custom-call(f32[4,24,384]{2,1,0:T(8,128)} %refs_0_.1, f32[3,8,8,128]{3,2,1,0:T(8,128)} %pad.4.refs_1_, f32[96,64]{1,0:T(8,128)} %constant.15.clone.refs_2_, f32[2,128,384]{2,1,0:T(8,128)} %constant.16.clone.refs_3_, f32[256,128]{1,0:T(8,128)} %constant.17.clone.refs_4_, f32[144,256]{1,0:T(8,128)} %constant.18.clone.refs_5_, ...), custom_call_target="tpu_custom_call" | custom-call | tf_op jit(solution)/shard_map/pallas_call | solution.py:352
  28.4 1.6 %copy.10 = f32[4,24,384]{2,1,0:T(8,128)} copy(f32[4,24,384]{2,1,0:T(8,128)} %shard_map.82) | data formatting | bytes 294912

commit v2 on v1

--- a/solution.py
+++ b/solution.py
@@ -97,9 +97,7 @@
 def constants(nz, gz, gy, yc, xc):
     bc = gz * xc // gy
     full = refine(gz * xc)
-    ex = np.zeros((gz, LANES, full.shape[1]), np.float32)
-    for h in range(gz):
-        ex[h, :xc] = full[h * xc : (h + 1) * xc]
+    ex = full.reshape(gz, xc, -1)
     block = refine_block(yc)
     rows = np.zeros((nz * 3 * yc, 2 * nz * yc), np.float32)
     for z in range(nz):
@@ -124,8 +122,8 @@
 
 
 def kernel(gz, gy, nz, yc, xc, *refs):
-    (scalar_hbm, vel, rows_hbm, ex_hbm, xy_hbm, xz_hbm, ey_hbm, eyt_hbm, out,
-     scalar, rows_m, ex_m, xy_m, xz_m, ey_m, eyt_m,
+    (scalar_hbm, vel_hbm, rows_hbm, ex_hbm, xy_hbm, xz_hbm, ey_hbm, eyt_hbm, out,
+     scalar, vel, rows_m, ex_m, xy_m, xz_m, ey_m, eyt_m,
      own, nxt, vsend, v0, v1, blocks, pencil, up_out, down_out, up_in, down_in,
      local_sem, own_s, own_r, nxt_s, nxt_r, v0_s, v0_r, v1_s, v1_r, blk_s, blk_r, z_s, z_r) = refs
     h = lax.axis_index("gz")
@@ -140,12 +138,25 @@
 
     loads = []
     for i, (src, dst) in enumerate((
-        (scalar_hbm, scalar), (rows_hbm, rows_m), (ex_hbm, ex_m), (xy_hbm, xy_m),
+        (vel_hbm, vel), (scalar_hbm, scalar), (rows_hbm, rows_m), (ex_hbm, ex_m), (xy_hbm, xy_m),
         (xz_hbm, xz_m), (ey_hbm, ey_m), (eyt_hbm, eyt_m),
     )):
         load = pltpu.make_async_copy(src, dst, local_sem.at[i])
         load.start()
         loads.append(load)
+
+    barrier = pltpu.get_barrier_semaphore()
+    everyone = gz * gy
+
+    def greet(i, _):
+        other = lax.rem(h * gy + s + i, everyone)
+        pl.semaphore_signal(
+            barrier, inc=1, device_id={"gz": other // gy, "gy": lax.rem(other, gy)},
+            device_id_type=pl.DeviceIdType.MESH,
+        )
+        return 0
+
+    lax.fori_loop(1, everyone, greet, 0)
 
     def remote(src, dst, send, recv, p, g):
         return pltpu.make_async_remote_copy(
@@ -163,16 +174,16 @@
         )
         return first, remote(planes, nxt.at[h], nxt_s.at[step], nxt_r.at[h], p, behind)
 
-    ux = [ux_copies(step) for step in range(gz)]
-    for first, second in ux:
-        second.start()
-        first.start()
-
+    loads[0].wait()
     lane = lax.broadcasted_iota(jnp.int32, (yc, LANES), 1)
+    fill = jnp.zeros((yc, LANES - xc), jnp.float32)
+    def wide_plane(value):
+        return jnp.concatenate([value, fill], axis=1)
+
     for p in range(gz):
-        planes = [vel[1, p * nz + z] for z in range(nz)]
+        planes = [wide_plane(vel[1, p * nz + z]) for z in range(nz)]
         for z in range(p * nz - 1, p * nz + nz + 1):
-            planes.append(vel[2, z] if 0 <= z < total else None)
+            planes.append(wide_plane(vel[2, z]) if 0 <= z < total else None)
         for c in range(per):
             tile = jnp.zeros((yc, LANES), jnp.float32)
             for i, plane in enumerate(planes):
@@ -182,6 +193,12 @@
                     )
             vsend[p, c] = tile
 
+    pl.semaphore_wait(barrier, everyone - 1)
+    ux = [ux_copies(step) for step in range(gz)]
+    for first, second in ux:
+        second.start()
+        first.start()
+
     def v_copies(which, n, act, own_too):
         dst_buf, send, recv, back = ((v0, v0_s, v0_r, 0), (v1, v1_s, v1_r, 1))[which]
         p = n // per
@@ -202,16 +219,15 @@
         for which in range(2):
             v_copies(which, n, lambda copy: copy.start(), True)
 
-    loads[0].wait()
-    loads[1].wait()
-    loads[2].wait()
+    for load in loads[1:4]:
+        load.wait()
     count = nz * yc
     speed = None
     for i in range(gz):
         pltpu.make_async_copy(own.at[i], own.at[i], own_r.at[i]).wait()
         pltpu.make_async_copy(nxt.at[i], nxt.at[i], nxt_r.at[i]).wait()
         coarse = jnp.concatenate(
-            [own[i].reshape(count, LANES), nxt[i].reshape(count, LANES)], axis=0
+            [own[i].reshape(count, xc), nxt[i].reshape(count, xc)], axis=0
         )
         part = dot(dot(rows_m[...], coarse), ex_m[i])
         speed = part if speed is None else speed + part
@@ -244,7 +260,7 @@
     for copy in sends[1:] + sends[:1]:
         copy.start()
 
-    for load in loads[3:]:
+    for load in loads[4:]:
         load.wait()
     for i in range(gy):
         pltpu.make_async_copy(v0.at[i], v0.at[i], v0_r.at[i]).wait()
@@ -327,18 +343,17 @@
     bc = gz * xc // gy
     bf = 3 * bc
     ny = gy * rf
-    vel = jnp.pad(velocity, ((0, 0), (0, 0), (0, 0), (0, LANES - xc)))
     mats = constants(nz, gz, gy, yc, xc)
     per = gy // gz
     f32 = jnp.float32
     dma = pltpu.SemaphoreType.DMA
     anywhere = pl.BlockSpec(memory_space=pl.ANY)
     vmem = pl.BlockSpec(memory_space=pltpu.VMEM)
-    scratch = [pltpu.VMEM(scalar.shape, f32)]
+    scratch = [pltpu.VMEM(scalar.shape, f32), pltpu.VMEM(velocity.shape, f32)]
     scratch += [pltpu.VMEM(m.shape, f32) for m in mats]
     scratch += [
-        pltpu.VMEM((gz, nz, yc, LANES), f32),
-        pltpu.VMEM((gz, nz, yc, LANES), f32),
+        pltpu.VMEM((gz, nz, yc, xc), f32),
+        pltpu.VMEM((gz, nz, yc, xc), f32),
         pltpu.VMEM((gz, per, yc, LANES), f32),
         pltpu.VMEM((gy, yc, LANES), f32),
         pltpu.VMEM((gy, yc, LANES), f32),
@@ -347,16 +362,16 @@
     ]
     scratch += [pltpu.VMEM((3, bf, ny), f32)] * 4
     scratch += [dma((n,)) for n in (
-        1 + len(mats), gz, gz, gz, gz, gz * per, gy, gz * per, gy, gy, gy, 2, 2
+        2 + len(mats), gz, gz, gz, gz, gz * per, gy, gz * per, gy, gy, gy, 2, 2
     )]
     return pl.pallas_call(
         functools.partial(kernel, gz, gy, nz, yc, xc),
-        out_shape=jax.ShapeDtypeStruct((nz, bf, ny), f32),
-        in_specs=[anywhere, vmem] + [anywhere] * len(mats),
+        out_shape=pltpu.VMEM((nz, bf, ny), f32),
+        in_specs=[anywhere] * (2 + len(mats)),
         out_specs=vmem,
         scratch_shapes=scratch,
-        compiler_params=pltpu.CompilerParams(has_side_effects=True),
-    )(scalar, vel, *[jnp.asarray(m) for m in mats])
+        compiler_params=pltpu.CompilerParams(has_side_effects=True, collective_id=0),
+    )(scalar, velocity, *[jnp.asarray(m) for m in mats])
 
 
 def solution(mesh):

time: 30.2 us -> 24.7 us (0.82)
  Pallas kernels: 26.9 us -> 23.9 us
  local copies, waits for them, and re-layouts: 3.12 us -> 0.66 us
    pallas_call x1, Pallas kernels: 26.9 us -> 23.9 us  [local(): pl.pallas_call(functools.partial(kernel, gz, gy, nz, yc, xc), out_shape=p...]
    pad x1 -> x0, local copies, waits for them, and re-layouts: 1.54 us -> none  [local(): vel = jnp.pad(velocity, ((0, 0), (0, 0), (0, 0), (0, LANES - xc)))]
    unnamed x1, local copies, waits for them, and re-layouts: 1.58 us -> 0.66 us
where the time goes in v2:
time: 24.7 us; the launch traced here: 24.6 us
  Pallas kernels  23.9 us (97%)
  local copies, waits for them, and re-layouts  0.66 us (3%)
    pallas_call x1, Pallas kernels, local(): pl.pallas_call(functools.partial(kernel, gz, gy, nz, yc, xc), out_shape=p...  23.9 us
    unnamed x1, local copies, waits for them, and re-layouts  0.66 us

profile of v2, /device:TPU:0, one launch (start us, length us, event | category | flops | bytes accessed | tf_op | source)
XLA Modules:
  0.0 24.6 jit_solution(16793914444641455526)
XLA Ops:
  0.0 23.9 %shard_map.82 = f32[4,24,384]{2,1,0:T(8,128)S(1)} custom-call(f32[4,24,384]{2,1,0:T(8,128)} %refs_0_.1, f32[3,8,8,64]{3,2,1,0:T(8,128)} %refs_1_.1, f32[96,64]{1,0:T(8,128)} %constant.12.clone.refs_2_, f32[2,64,384]{2,1,0:T(8,128)} %constant.13.clone.refs_3_, f32[256,128]{1,0:T(8,128)} %constant.14.clone.refs_4_, f32[144,256]{1,0:T(8,128)} %constant.15.clone.refs_5_, ...), custom_call_target="tpu_custom_call" | custom-call | tf_op jit(solution)/shard_map/pallas_call | solution.py:367
  23.9 0.7 %copy.10 = f32[4,24,384]{2,1,0:T(8,128)} copy(f32[4,24,384]{2,1,0:T(8,128)S(1)} %shard_map.82) | data formatting | bytes 294912

commit v3 on v2

--- a/solution.py
+++ b/solution.py
@@ -110,15 +110,20 @@
     xz = np.zeros(((nz + 2) * 3 * bc, 2 * LANES), np.float32)
     for plane in range(planes):
         for part in range(2):
-            at = part * LANES + plane * bc
-            piece = block[part * bc : (part + 1) * bc]
+            at = part * LANES + plane * (bc + 1)
+            piece = block[bc : bc + 1] if part else block[: bc + 1]
+            end = at + len(piece)
             if plane < nz:
-                xy[at : at + bc, plane * 3 * bc : (plane + 1) * 3 * bc] = piece
+                xy[at:end, plane * 3 * bc : (plane + 1) * 3 * bc] = piece
             else:
                 z = plane - nz
-                xz[z * 3 * bc : (z + 1) * 3 * bc, at : at + bc] = piece.T
+                xz[z * 3 * bc : (z + 1) * 3 * bc, at:end] = piece.T
     ey = refine(gy * yc)
     return rows, ex, xy, xz, ey, np.ascontiguousarray(ey.T)
+
+
+def wrapped(index, size):
+    return jnp.where(index >= size, index - size, index)
 
 
 def kernel(gz, gy, nz, yc, xc, *refs):
@@ -132,8 +137,8 @@
     bc = gz * xc // gy
     bf = 3 * bc
     per = gy // gz
-    ahead = lax.rem(s + 1, gy)
-    behind = lax.rem(s + gy - 1, gy)
+    behind = wrapped(s + gy - 1, gy)
+    at_end = lax.rem(s, per) == per - 1
     total = gz * nz
 
     loads = []
@@ -148,15 +153,20 @@
     barrier = pltpu.get_barrier_semaphore()
     everyone = gz * gy
 
-    def greet(i, _):
-        other = lax.rem(h * gy + s + i, everyone)
+    def greet(step, p):
         pl.semaphore_signal(
-            barrier, inc=1, device_id={"gz": other // gy, "gy": lax.rem(other, gy)},
+            barrier, inc=1, device_id={"gz": p, "gy": wrapped(s + step, gy)},
             device_id_type=pl.DeviceIdType.MESH,
         )
+
+    def greet_all(step, _):
+        for i in range(gz):
+            greet(step, wrapped(h + i, gz))
         return 0
 
-    lax.fori_loop(1, everyone, greet, 0)
+    for i in range(1, gz):
+        greet(0, wrapped(h + i, gz))
+    lax.fori_loop(1, gy, greet_all, 0, unroll=gz * gy <= 64)
 
     def remote(src, dst, send, recv, p, g):
         return pltpu.make_async_remote_copy(
@@ -165,7 +175,7 @@
         )
 
     def ux_copies(step):
-        p = lax.rem(h + step, gz)
+        p = wrapped(h + step, gz)
         planes = vel.at[0, pl.ds(p * nz, nz)]
         first = (
             pltpu.make_async_copy(planes, own.at[h], own_r.at[h])
@@ -189,9 +199,16 @@
             for i, plane in enumerate(planes):
                 if plane is not None:
                     tile = jnp.where(
-                        (lane >= i * bc) & (lane < (i + 1) * bc), roll(plane, (i - c) * bc, 1), tile
+                        (lane >= i * (bc + 1)) & (lane < i * (bc + 1) + min(bc + 1, xc - c * bc)),
+                        roll(plane, i * (bc + 1) - c * bc, 1),
+                        tile,
                     )
             vsend[p, c] = tile
+
+
+    @pl.when(jnp.logical_not(at_end))
+    def _():
+        v1[...] = jnp.zeros(v1.shape, jnp.float32)
 
     pl.semaphore_wait(barrier, everyone - 1)
     ux = [ux_copies(step) for step in range(gz)]
@@ -199,25 +216,26 @@
         second.start()
         first.start()
 
-    def v_copies(which, n, act, own_too):
-        dst_buf, send, recv, back = ((v0, v0_s, v0_r, 0), (v1, v1_s, v1_r, 1))[which]
-        p = n // per
-        c = n % per
-        g = lax.rem(h * per + c + gy - back, gy)
+    def v_copies(p, c, first, act, own_too):
+        if first:
+            dst_buf, send, recv, g = v0, v0_s.at[p * per + c], v0_r, h * per + c
+        else:
+            dst_buf, send, recv, g = v1, v1_s.at[p], v1_r, wrapped(h * per + c + gy - 1, gy)
         mine = (p == h) & (g == s)
 
         @pl.when(jnp.logical_not(mine))
         def _():
-            act(remote(vsend.at[p, c], dst_buf.at[s], send.at[n], recv.at[s], p, g))
+            act(remote(vsend.at[p, c], dst_buf.at[s], send, recv.at[s], p, g))
 
         if own_too:
             @pl.when(mine)
             def _():
                 act(pltpu.make_async_copy(vsend.at[p, c], dst_buf.at[s], recv.at[s]))
 
-    for n in range(gz * per):
-        for which in range(2):
-            v_copies(which, n, lambda copy: copy.start(), True)
+    v_tiles = [(p, c, first) for p in range(gz) for first in (True, False)
+               for c in (range(per) if first else range(1))]
+    for p, c, first in v_tiles:
+        v_copies(p, c, first, lambda copy: copy.start(), True)
 
     for load in loads[1:4]:
         load.wait()
@@ -251,7 +269,7 @@
         blocks[g] = tile
 
     def block_copy(step):
-        g = lax.rem(s + step, gy)
+        g = wrapped(s + step, gy)
         if step == 0:
             return pltpu.make_async_copy(blocks.at[g], pencil.at[s], blk_r.at[s])
         return remote(blocks.at[g], pencil.at[s], blk_s.at[step], blk_r.at[s], h, g)
@@ -264,7 +282,12 @@
         load.wait()
     for i in range(gy):
         pltpu.make_async_copy(v0.at[i], v0.at[i], v0_r.at[i]).wait()
-        pltpu.make_async_copy(v1.at[i], v1.at[i], v1_r.at[i]).wait()
+
+    @pl.when(at_end)
+    def _():
+        for i in range(gy):
+            pltpu.make_async_copy(v1.at[i], v1.at[i], v1_r.at[i]).wait()
+
     nyc = gy * yc
     coarse = jnp.concatenate(
         [v0[...].reshape(nyc, LANES), v1[...].reshape(nyc, LANES)], axis=1
@@ -277,53 +300,66 @@
     field = pencil[...].reshape(gy * rf, LANES)
     field = sweep_periodic(field, speed_y, 0)
 
-    field = jnp.transpose(field)[: nz * bf]
-    moved = displacement(
-        speed_z[bf : (nz + 1) * bf], speed_z[: nz * bf], speed_z[2 * bf : (nz + 2) * bf]
-    )
-    w = weights(moved)
-
-    def landing(target):
-        result = None
-        for m in range(-3, 4):
-            z = target - m
-            if 0 <= z < nz:
-                at = slice(z * bf, (z + 1) * bf)
-                term = field[at] * w[m][at]
-                result = term if result is None else result + term
-        return result
-
-    for i in range(3):
-        up_out[i] = landing(nz + i)
-        down_out[i] = landing(i - 3)
-
-    up = remote(up_out, up_in, z_s.at[0], z_r.at[0], lax.rem(h + 1, gz), s)
-    down = remote(down_out, down_in, z_s.at[1], z_r.at[1], lax.rem(h + gz - 1, gz), s)
+    ny = gy * rf
+    chunks = ny // LANES
+    below, above = wrapped(h + gz - 1, gz), wrapped(h + 1, gz)
+    ups, downs = [], []
+    for k in range(chunks):
+        cols = slice(k * LANES, (k + 1) * LANES)
+        part = jnp.transpose(field[cols])[: nz * bf]
+        moved = displacement(
+            speed_z[bf : (nz + 1) * bf, cols], speed_z[: nz * bf, cols], speed_z[2 * bf :, cols]
+        )
+        w = weights(moved)
+
+        def landing(target):
+            result = None
+            for m in range(-3, 4):
+                z = target - m
+                if 0 <= z < nz:
+                    at = slice(z * bf, (z + 1) * bf)
+                    term = part[at] * w[m][at]
+                    result = term if result is None else result + term
+            return result
+
+        for i in range(3):
+            up_out[k, i] = landing(nz + i)
+            down_out[k, i] = landing(i - 3)
+        up = remote(up_out.at[k], up_in.at[k], z_s.at[0, k], z_r.at[0, k], above, s)
+        down = remote(down_out.at[k], down_in.at[k], z_s.at[1, k], z_r.at[1, k], below, s)
+        ups.append(up)
+        downs.append(down)
+
+        @pl.when(h < gz - 1)
+        def _():
+            up.start()
+
+        @pl.when(h > 0)
+        def _():
+            down.start()
+
+        for i in range(nz):
+            out[i, :, cols] = landing(i)
+
+    @pl.when(h > 0)
+    def _():
+        for k in range(chunks):
+            cols = slice(k * LANES, (k + 1) * LANES)
+            ups[k].wait_recv()
+            for i in range(3):
+                out[i, :, cols] = out[i, :, cols] + up_in[k, i]
+        for copy in downs:
+            copy.wait_send()
 
     @pl.when(h < gz - 1)
     def _():
-        up.start()
-
-    @pl.when(h > 0)
-    def _():
-        down.start()
-
-    for i in range(nz):
-        out[i] = landing(i)
-
-    @pl.when(h > 0)
-    def _():
-        up.wait_recv()
-        for i in range(3):
-            out[i] = out[i] + up_in[i]
-        down.wait_send()
-
-    @pl.when(h < gz - 1)
-    def _():
-        down.wait_recv()
-        for i in range(3):
-            out[nz - 3 + i] = out[nz - 3 + i] + down_in[i]
-        up.wait_send()
+        for k in range(chunks):
+            cols = slice(k * LANES, (k + 1) * LANES)
+            downs[k].wait_recv()
+            for i in range(nz - 3, nz):
+                out[i, :, cols] = out[i, :, cols] + down_in[k, i - nz + 3]
+        for copy in ups:
+            copy.wait_send()
 
     for step, (first, second) in enumerate(ux):
         if step:
@@ -331,9 +367,8 @@
         second.wait_send()
     for copy in sends[1:]:
         copy.wait_send()
-    for n in range(gz * per):
-        for which in range(2):
-            v_copies(which, n, lambda copy: copy.wait_send(), False)
+    for p, c, first in v_tiles:
+        v_copies(p, c, first, lambda copy: copy.wait_send(), False)
 
 
 def local(scalar, velocity):
@@ -360,10 +395,11 @@
         pltpu.VMEM((gy, rf, LANES), f32),
         pltpu.VMEM((gy, rf, LANES), f32),
     ]
-    scratch += [pltpu.VMEM((3, bf, ny), f32)] * 4
+    scratch += [pltpu.VMEM((ny // LANES, 3, bf, LANES), f32)] * 4
     scratch += [dma((n,)) for n in (
-        2 + len(mats), gz, gz, gz, gz, gz * per, gy, gz * per, gy, gy, gy, 2, 2
+        2 + len(mats), gz, gz, gz, gz, gz * per, gy, gz, gy, gy, gy
     )]
+    scratch += [dma((2, ny // LANES))] * 2
     return pl.pallas_call(
         functools.partial(kernel, gz, gy, nz, yc, xc),
         out_shape=pltpu.VMEM((nz, bf, ny), f32),

time: 24.7 us -> 23.3 us (0.943)
  Pallas kernels: 23.9 us -> 22.5 us
    pallas_call x1, Pallas kernels: 23.9 us -> 22.5 us  [local(): pl.pallas_call(functools.partial(kernel, gz, gy, nz, yc, xc), out_shape=p...]
where the time goes in v3:
time: 23.3 us; the launch traced here: 23.2 us
  Pallas kernels  22.5 us (97%)
  local copies, waits for them, and re-layouts  0.66 us (3%)
    pallas_call x1, Pallas kernels, local(): pl.pallas_call(functools.partial(kernel, gz, gy, nz, yc, xc), out_shape=p...  22.5 us
    unnamed x1, local copies, waits for them, and re-layouts  0.66 us

profile of v3, /device:TPU:0, one launch (start us, length us, event | category | flops | bytes accessed | tf_op | source)
XLA Modules:
  0.0 23.2 jit_solution(5871814273596881412)
XLA Ops:
  0.0 22.5 %shard_map.82 = f32[4,24,384]{2,1,0:T(8,128)S(1)} custom-call(f32[4,24,384]{2,1,0:T(8,128)} %refs_0_.1, f32[3,8,8,64]{3,2,1,0:T(8,128)} %refs_1_.1, f32[96,64]{1,0:T(8,128)} %constant.12.clone.refs_2_, f32[2,64,384]{2,1,0:T(8,128)} %constant.13.clone.refs_3_, f32[256,128]{1,0:T(8,128)} %constant.14.clone.refs_4_, f32[144,256]{1,0:T(8,128)} %constant.15.clone.refs_5_, ...), custom_call_target="tpu_custom_call" | custom-call | tf_op jit(solution)/shard_map/pallas_call | solution.py:403
  22.5 0.7 %copy.10 = f32[4,24,384]{2,1,0:T(8,128)} copy(f32[4,24,384]{2,1,0:T(8,128)S(1)} %shard_map.82) | data formatting | bytes 294912
